TPU v7x, 512 devices: a whole 4x4x16 slice. The times are simulated.
512 devices in a mesh: row: 16 (over x, y), col: 32 (over z, core).
Axes of the slice: x: 4, y: 4, z: 16, core: 2. Of those that a mesh axis runs over, the one named last changes fastest.
Arguments:
- gradient: float32 [5504, 4096], P('col', 'row'), may hold values from -6 to 6
- ginv: float32 [5504, 5504], P('col', 'row'), may hold values from -1 to 3.5, as said below
- ainv: float32 [4096, 4096], P('col', 'row'), may hold values from -1 to 3.5, as said below
Outputs:
- preconditioned: float32 [5504, 4096], P('col', 'row')
Inputs may be any that keep to these rules, and one draw needn't show every extreme that they name: ginv is exactly symmetric and positive definite. ainv is exactly symmetric and positive definite.
All inputs are finite; a program needn't handle non-finite values.
Results may differ from a plain program's by a relative error of at most 0.000086.
Values sent between devices are 32-bit elements; how exact they have to be, the bound alone decides.
A program may use at most 64 MiB of HBM per device.

v0:
```python
import jax
import jax.numpy as jnp
from jax import lax
from jax.sharding import PartitionSpec as P

highest_mode = lax.Precision.HIGHEST


def joined_along(tiles, dim):
    dims = list(tiles.shape[1:])
    dims[dim] *= tiles.shape[0]
    return jnp.moveaxis(tiles, 0, dim).reshape(dims)


def from_everyone(shard, axis):
    devices = lax.axis_size(axis)
    return lax.all_to_all(
        jnp.broadcast_to(shard[None], (devices, *shard.shape)), axis, 0, 0, tiled=True
    )


def gather_directly(shard, axis, dim):
    return joined_along(from_everyone(shard, axis), dim)


def body(gradient, ginv, ainv):
    grad_whole = lax.all_gather(gradient, "col", axis=0, tiled=True)
    rows_part = grad_whole
    left = jnp.dot(
        gather_directly(ginv, "row", 1),
        rows_part,
        precision=highest_mode,
        preferred_element_type=jnp.float32,
    )
    ainv_whole = lax.all_gather(ainv, "col", axis=0, tiled=True)
    rows_part = ainv_whole
    return jnp.dot(
        gather_directly(left, "row", 1),
        rows_part,
        precision=highest_mode,
        preferred_element_type=jnp.float32,
    )


def solution(mesh):
    return jax.shard_map(
        body,
        mesh=mesh,
        in_specs=(P("col", "row"), P("col", "row"), P("col", "row")),
        out_specs=P("col", "row"),
        check_vma=False,
    )
```

profile of v0, /device:TPU:1, one launch (start us, length us, event | category | flops | bytes accessed | tf_op | source)
XLA Modules:
  0.0 174.9 jit_solution(1155137543293335486)
XLA Ops:
  6.5 0.0 all-gather.6.cloned.1.call-start
  6.5 0.7 all-gather.6.cloned.1.call-update
  7.3 0.0 all-gather.4.cloned.1.call-start
  7.3 0.7 all-gather.4.cloned.1.call-update
  8.0 1.2 broadcast_in_dim.4
  9.2 57.3 %all_to_all.10 = f32[16,172,344]{2,1,0:T(8,128)S(1)} all-to-all(f32[16,172,344]{2,1,0:T(8,128)S(1)} %broadcast_in_dim.4), channel_id=1, replica_groups=mesh['row'=16,'col'=32] {'row'}, dimensions={0} | all-to-all | bytes 7573504 | tf_op jit(solution)/shard_map/all_to_all | solution.py:17
  66.5 3.3 %copy.4 = f32[172,16,344]{2,1,0:T(8,128)} copy(f32[172,16,344]{2,0,1:T(8,128)S(1)} %bitcast.10) | data formatting | bytes 7573504 | tf_op jit(solution)/shard_map/transpose | solution.py:12
  69.8 5.6 %reshape.8 = f32[172,5504]{1,0:T(8,128)} reshape(f32[172,16,344]{2,1,0:T(8,128)} %copy.4) | data formatting | bytes 7573504 | tf_op jit(solution)/shard_map/reshape | solution.py:12
  75.4 15.0 %all-gather.6.cloned.1.call-done = f32[32,172,256]{2,1,0:T(8,128)} async-done(((f32[1,172,256]{2,1,0:T(8,128)}), f32[32,172,256]{2,1,0:T(8,128)}) %all-gather.6.cloned.1.call-update) | async-done | bytes 5636112 | tf_op jit(solution)/shard_map/all_gather | solution.py:27
  90.4 6.8 %reshape.11 = f32[5504,256]{1,0:T(8,128)} reshape(f32[32,172,256]{2,1,0:T(8,128)} %all-gather.6.cloned.1.call-done) | data formatting | bytes 11272192
  97.2 7.4 %fusion = f32[172,256]{1,0:T(8,128)S(1)} fusion(f32[172,5504]{1,0:T(8,128)} %reshape.8, f32[5504,256]{1,0:T(8,128)} %reshape.11), kind=kOutput, calls=%fused_computation | convolution fusion | flops 2908225536 | bytes 9598976 | tf_op jit(solution)/shard_map/dot_general | solution.py:29
  104.6 0.3 broadcast_in_dim.5
  104.8 42.4 %all_to_all.11 = f32[16,172,256]{2,1,0:T(8,128)S(1)} all-to-all(f32[16,172,256]{2,1,0:T(8,128)S(1)} %broadcast_in_dim.5), channel_id=1, replica_groups=mesh['row'=16,'col'=32] {'row'}, dimensions={0} | all-to-all | bytes 5636096 | tf_op jit(solution)/shard_map/all_to_all | solution.py:17
  147.2 1.6 copy.5
  148.9 0.3 pad
  149.1 2.4 %copy.6 = f32[22,8,16,256]{3,1,2,0:T(8,128)S(1)} copy(f32[22,8,16,256]{3,2,1,0:T(8,128)S(1)} %bitcast.12) | data formatting | bytes 5767168
  151.6 10.9 %all-gather.4.cloned.1.call-done = f32[4096,256]{1,0:T(8,128)} async-done(((f32[128,256]{1,0:T(8,128)}), f32[4096,256]{1,0:T(8,128)}) %all-gather.4.cloned.1.call-update) | async-done | bytes 4194320 | tf_op jit(solution)/shard_map/all_gather | solution.py:35
  162.5 5.5 %fusion.1 = f32[172,256]{1,0:T(8,128)} fusion(f32[172,4096]{1,0:T(8,128)S(1)} %bitcast.11, f32[4096,256]{1,0:T(8,128)} %all-gather.4.cloned.1.call-done), kind=kOutput, calls=%fused_computation.1 | convolution fusion | flops 2164260864 | bytes 7188480 | tf_op jit(solution)/shard_map/dot_general | solution.py:37
Async XLA Ops:
  6.5 83.9 %all-gather.6.cloned.1.call-start = ((), (), s32[]{:S(2)}) async-start(), calls=%async_computation.3 | async-start | bytes 5947392 | tf_op jit(solution)/shard_map/all_gather | solution.py:27
  7.3 155.3 %all-gather.4.cloned.1.call-start = ((), (), s32[]{:S(2)}) async-start(), calls=%async_computation.2 | async-start | bytes 4325376 | tf_op jit(solution)/shard_map/all_gather | solution.py:35
Sparse Core Ops, SparseCore 0:
  9.5 80.9 all-gather.5
  92.5 69.9 all-gather.3
where the time goes:
time: 175 us
  blocking collectives  99.7 us (57%)
  waiting for transfers between devices  27.3 us (16%)
  local copies, waits for them, and re-layouts  21.5 us (12%)
  between operations  13.4 us (8%)
  matrix products  12.9 us (7%)
    all_to_all x2, blocking collectives, from_everyone(): lax.all_to_all(jnp.broadcast_to(shard[None], (devices, *shard.shape)), ax...  99.7 us
    all_gather x1, waiting for transfers between devices, body(): grad_whole = lax.all_gather(gradient, 'col', axis=0, tiled=True)  15 us
    all_gather x1, waiting for transfers between devices, body(): ainv_whole = lax.all_gather(ainv, 'col', axis=0, tiled=True)  10.9 us
    unnamed x3, local copies, waits for them, and re-layouts  9.49 us
    dot_general x1, matrix products, body(): jnp.dot(gather_directly(ginv, 'row', 1), rows_part, precision=highest_mod...  7.36 us
    reshape x1, local copies, waits for them, and re-layouts, joined_along(): return jnp.moveaxis(tiles, 0, dim).reshape(dims)  5.59 us
    dot_general x1, matrix products, body(): jnp.dot(gather_directly(left, 'row', 1), rows_part, precision=highest_mod...  5.54 us
    transpose x2, local copies, waits for them, and re-layouts, joined_along(): return jnp.moveaxis(tiles, 0, dim).reshape(dims)  4.95 us
  transfers between devices with their start and end apart: 2, of which 2 were waited for; matrix products, arithmetic and copies ran while one was open for 17% of the time, Pallas kernels for 0%

commit v1 on v0

v1 whole, which is shorter than its diff:
```python
import functools
import heapq

import jax
import jax.numpy as jnp
from jax import lax
from jax.experimental import pallas as pl
from jax.experimental.pallas import tpu as pltpu
from jax.sharding import PartitionSpec as P

MESH = pl.DeviceIdType.MESH
F32 = jnp.float32
BF16 = jnp.bfloat16

X = 4
Z = 16
M = 172
MP = 176
HM = MP // 2
N = 256
NA = 128
KV = 344
KP = 384
PIECES = {"A": 2, "T": 2}
PART = {"A": NA, "T": MP}
LIMIT = (8, 7)
UNITS = (0, -1, 1, 2)
GOES_RIGHT = (0, -1)
TURN = {"G": "right", "V": "left"}


def plane_index(u, v):
    return UNITS.index(u) * 4 + UNITS.index(v)


def plan():
    rate = 90e3
    hop, near, turn = 1.9, 1.0, 0.1
    size = {"G": HM * N * 4, "V": HM * KP * 4, "A": NA * N * 4, "T": MP * N * 4}
    free = {}
    heap = []
    order = []
    count = [0]

    def send(now, link, nbytes, event):
        start = max(now, free.get(link, 0.0))
        pace = 500e3 if link == "d" else rate
        free[link] = start + nbytes / pace
        count[0] += 1
        heapq.heappush(heap, (free[link] + (near if link == "d" else hop), count[0], event))

    def axes(h):
        return ("x", "y") if h == 0 else ("y", "x")

    def plane_send(now, q, h, axis, way, event):
        send(now, axis + way, 2 * size[q], event)

    def plane_own(now, q):
        for h in (0, 1):
            first, second = axes(h)
            plane_send(now, q, h, first, "+", (q, h, -1, 0))
            plane_send(now, q, h, first, "-", (q, h, 1, 0))
        for h in (0, 1):
            first, second = axes(h)
            plane_send(now, q, h, second, "+", (q, h, 0, -1))
            plane_send(now, q, h, second, "-", (q, h, 0, 1))

    def ring_own(now, q):
        for k in range(PIECES[q]):
            send(now, "z", size[q] / PIECES[q], (q, 1, 0, k))
            send(now, "d", size[q] / PIECES[q], (q, 0, 1, k))

    def act(now, event):
        q = event[0]
        if q in "GV":
            _, h, u, v = event
            first, second = axes(h)
            if v == 0:
                if u == -1 and TURN[q] == "right":
                    plane_send(now, q, h, first, "+", (q, h, 2, 0))
                if u == 1 and TURN[q] == "left":
                    plane_send(now, q, h, first, "-", (q, h, 2, 0))
                plane_send(now, q, h, second, "+", (q, h, u, -1))
                plane_send(now, q, h, second, "-", (q, h, u, 1))
            if v == -1 and u in GOES_RIGHT:
                plane_send(now, q, h, second, "+", (q, h, u, 2))
            if v == 1 and u not in GOES_RIGHT:
                plane_send(now, q, h, second, "-", (q, h, u, 2))
        else:
            _, s, p, k = event
            if s < LIMIT[p]:
                send(now, "z", size[q] / PIECES[q], (q, s + 1, p, k))
            if s > 0:
                send(now, "d", size[q] / PIECES[q], ("sibling",))

    plane_own(0.0, "G")
    ring_own(0.0, "A")
    left = {"G": 30, "A": 16 * PIECES["A"], "V": 30, "T": 16 * PIECES["T"]}
    early = 8
    pending = []
    while heap:
        now, _, event = heapq.heappop(heap)
        if event[0] == "sibling":
            continue
        order.append((now, event))
        act(now + turn, event)
        q = event[0]
        left[q] -= 1
        if q == "G" and left[q] == early:
            plane_own(now + turn, "V")
            order.append((now, ("begin", "V")))
        if q in "AG" and left["A"] == 0 and left["G"] == 0:
            ring_own(now + 2.0, "T")
            order.append((now, ("begin", "T")))
    return order


def split(x):
    high = x.astype(BF16)
    return high, (x - high.astype(F32)).astype(BF16)


def product(a, b):
    a1, a2 = split(a)
    b1, b2 = split(b)
    dot = functools.partial(jnp.dot, preferred_element_type=F32)
    return dot(a1, b2) + dot(a2, b1) + dot(a1, b1)


def kernel(
    grad_ref, ginv_ref, ainv_ref, out_ref,
    gbuf, vbuf, abuf, tbuf, acc, gstage, vstage, local,
    g_send, g_recv, v_send, v_recv, az_send, az_recv, as_send, as_recv, tz_send, tz_recv, ts_send, ts_recv,
):
    r, c = lax.axis_index("row"), lax.axis_index("col")
    x, y = r // X, lax.rem(r, X)
    z, core = c // 2, lax.rem(c, 2)
    other = 1 - core
    way = 1 - 2 * core

    def at_xy(dx, dy):
        return lax.rem(x + dx + X, X) * X + lax.rem(y + dy + X, X)

    def at_z(d):
        return lax.rem(z + d + Z, Z)

    ahead = (r, at_z(way) * 2 + core)
    behind = (r, at_z(-way) * 2 + core)
    sibling = (r, z * 2 + other)
    side = {
        ("x", 1): (at_xy(1, 0), c),
        ("x", -1): (at_xy(-1, 0), c),
        ("y", 1): (at_xy(0, 1), c),
        ("y", -1): (at_xy(0, -1), c),
    }

    loads = [
        pltpu.make_async_copy(grad_ref, gstage, local.at[0]),
        pltpu.make_async_copy(ginv_ref, vstage, local.at[1]),
        pltpu.make_async_copy(ainv_ref, abuf.at[z, pl.ds(pl.multiple_of(core * NA, NA), NA)], local.at[2]),
    ]
    for load in loads:
        load.start()
    barrier = pltpu.get_barrier_semaphore()
    peers = [ahead, behind, sibling, *side.values()]
    for peer in peers:
        pl.semaphore_signal(barrier, inc=1, device_id=peer, device_id_type=MESH)

    loads[0].wait()
    gbuf[r, 0:M, :] = gstage[...]
    gbuf[r, M:MP, :] = jnp.zeros((MP - M, N), F32)
    loads[1].wait()
    vbuf[r] = jnp.zeros((MP, KP), F32)
    vbuf[r, 0:M, 0:M] = vstage[:, 0:M]
    vbuf[r, 0:M, MP : MP + M] = vstage[:, M:KV]
    acc[...] = jnp.zeros_like(acc)
    loads[2].wait()
    pl.semaphore_wait(barrier, len(peers))

    plane = {"G": (gbuf, g_send, g_recv), "V": (vbuf, v_send, v_recv)}
    ring = {
        "A": (abuf, az_send, az_recv, as_send, as_recv),
        "T": (tbuf, tz_send, tz_recv, ts_send, ts_recv),
    }
    sent = []

    def origin(h, u, v):
        return at_xy(u, v) if h == 0 else at_xy(v, u)

    def plane_copy(q, h, u, v, to, ru, rv):
        buf, send_sem, recv_sem = plane[q]
        piece = buf.at[origin(h, u, v), pl.ds(h * HM, HM)]
        i = h * 16 + plane_index(ru, rv)
        copy = pltpu.make_async_remote_copy(
            piece, piece, send_sem.at[i], recv_sem.at[i], device_id=to, device_id_type=MESH
        )
        copy.start()
        sent.append(copy)

    def plane_wait(q, h, u, v):
        buf, send_sem, recv_sem = plane[q]
        piece = buf.at[origin(h, u, v), pl.ds(h * HM, HM)]
        i = h * 16 + plane_index(u, v)
        pltpu.make_async_remote_copy(
            piece, piece, send_sem.at[i], recv_sem.at[i], device_id=sibling, device_id_type=MESH
        ).wait_recv()

    def axes(h):
        return ("x", "y") if h == 0 else ("y", "x")

    def across(q, h, u):
        second = axes(h)[1]
        plane_copy(q, h, u, 0, side[second, 1], u, -1)
        plane_copy(q, h, u, 0, side[second, -1], u, 1)

    def plane_own(q):
        for h in (0, 1):
            first = axes(h)[0]
            plane_copy(q, h, 0, 0, side[first, 1], -1, 0)
            plane_copy(q, h, 0, 0, side[first, -1], 1, 0)
        for h in (0, 1):
            across(q, h, 0)

    def plane_event(q, h, u, v):
        plane_wait(q, h, u, v)
        first, second = axes(h)
        if v == 0:
            if u == -1 and TURN[q] == "right":
                plane_copy(q, h, u, 0, side[first, 1], 2, 0)
            if u == 1 and TURN[q] == "left":
                plane_copy(q, h, u, 0, side[first, -1], 2, 0)
            across(q, h, u)
        if v == -1 and u in GOES_RIGHT:
            plane_copy(q, h, u, v, side[second, 1], u, 2)
        if v == 1 and u not in GOES_RIGHT:
            plane_copy(q, h, u, v, side[second, -1], u, 2)

    def piece_of(q, owner, part, k):
        rows = PART[q] // PIECES[q]
        start = pl.multiple_of(part * PART[q] + k * rows, 8)
        return ring[q][0].at[owner, pl.ds(start, rows)]

    def index(q, s, p, k):
        return (s * 2 + p) * PIECES[q] + k

    def ring_block(q, s, p, k):
        return piece_of(q, at_z(-way * s), core if p == 0 else other, k)

    def sibling_block(q, s, p, k):
        return piece_of(q, at_z(way * s), other if p == 0 else core, k)

    def forward(q, s, p, k):
        _, zs, zr, _, _ = ring[q]
        piece = ring_block(q, s, p, k)
        i = index(q, s + 1, p, k)
        copy = pltpu.make_async_remote_copy(piece, piece, zs.at[i], zr.at[i], device_id=ahead, device_id_type=MESH)
        copy.start()
        sent.append(copy)

    def hand_over(q, s, p, k):
        _, _, _, ss, sr = ring[q]
        piece = ring_block(q, s, p, k)
        i = index(q, s, p, k)
        copy = pltpu.make_async_remote_copy(piece, piece, ss.at[i], sr.at[i], device_id=sibling, device_id_type=MESH)
        copy.start()
        sent.append(copy)

    def ring_own(q):
        for k in range(PIECES[q]):
            forward(q, 0, 0, k)
            hand_over(q, 0, 0, k)

    def ring_event(q, s, p, k):
        _, zs, zr, ss, sr = ring[q]
        if s == 0:
            wait_sibling(q, 0, 0, k)
        else:
            piece = ring_block(q, s, p, k)
            i = index(q, s, p, k)
            pltpu.make_async_remote_copy(
                piece, piece, zs.at[i], zr.at[i], device_id=sibling, device_id_type=MESH
            ).wait_recv()
        if s < LIMIT[p]:
            forward(q, s, p, k)
        if s > 0:
            hand_over(q, s, p, k)

    def wait_sibling(q, s, p, k):
        _, _, _, ss, sr = ring[q]
        piece = sibling_block(q, s, p, k)
        i = index(q, s, p, k)
        pltpu.make_async_remote_copy(
            piece, piece, ss.at[i], sr.at[i], device_id=sibling, device_id_type=MESH
        ).wait_recv()

    def grad_dot(owner):
        acc[...] += product(gbuf[owner], abuf[owner])

    def ginv_dot(owner):
        acc[...] += product(vbuf[owner][:, 0 : 2 * MP], tbuf[owner])

    dots = {"A": grad_dot, "T": ginv_dot}

    def do_dot(q, e):
        if 0 < e < 8:
            for k in range(PIECES[q]):
                wait_sibling(q, e, 0, k)
                wait_sibling(q, e, 1, k)
        if e == 8:
            for k in range(PIECES[q]):
                wait_sibling(q, 8, 0, k)
        dots[q](at_z(way * e))

    plane_own("G")
    ring_own("A")
    left = {"G": 30, "V": 30}
    ready = []
    seen = {}

    def drain(q, at_most):
        for _ in range(min(at_most, len(ready))):
            do_dot(q, ready.pop(0))

    def note_ring(q, s, p):
        seen[q, s] = seen.get((q, s), 0) + 1
        if s == 8:
            if seen[q, s] == PIECES[q]:
                ready.append(8)
        elif s == 0:
            if seen[q, s] == PIECES[q]:
                ready.append(0)
        elif seen[q, s] == 2 * PIECES[q]:
            ready.extend([-s, s])

    for _, event in plan():
        q = event[0]
        if q == "begin":
            if event[1] == "V":
                plane_own("V")
            else:
                drain("A", len(ready))
                tbuf[z, pl.ds(pl.multiple_of(core * MP, 8), MP), :] = acc[...]
                ring_own("T")
                acc[...] = jnp.zeros_like(acc)
        elif q in "GV":
            plane_event(*event)
            left[q] -= 1
            if q == "G" and left["G"] == 0:
                pass
        else:
            ring_event(*event)
            note_ring(q, event[1], event[2])
            if q == "A" and left["G"] == 0 or q == "T" and left["V"] == 0:
                drain(q, 3)
    drain("T", len(ready))
    out_ref[...] = acc[0:M, :]
    for copy in sent:
        copy.wait_send()


def body(gradient, ginv, ainv):
    na, nt = 18 * PIECES["A"], 18 * PIECES["T"]
    sem = pltpu.SemaphoreType.DMA
    return pl.pallas_call(
        kernel,
        name="precondition",
        out_shape=jax.ShapeDtypeStruct((M, N), F32),
        in_specs=[pl.BlockSpec(memory_space=pl.ANY)] * 3,
        out_specs=pl.BlockSpec(memory_space=pltpu.VMEM),
        scratch_shapes=[
            pltpu.VMEM((X * X, MP, N), F32),
            pltpu.VMEM((X * X, MP, KP), F32),
            pltpu.VMEM((Z, 2 * NA, N), F32),
            pltpu.VMEM((Z, 2 * MP, N), F32),
            pltpu.VMEM((MP, N), F32),
            pltpu.VMEM((M, N), F32),
            pltpu.VMEM((M, KV), F32),
            sem((3,)),
            sem((32,)),
            sem((32,)),
            sem((32,)),
            sem((32,)),
            *[sem((na,))] * 4,
            *[sem((nt,))] * 4,
        ],
        compiler_params=pltpu.CompilerParams(
            collective_id=0, has_side_effects=True, vmem_limit_bytes=60 * 1024 * 1024
        ),
    )(gradient, ginv, ainv)


def solution(mesh):
    return jax.shard_map(
        body,
        mesh=mesh,
        in_specs=(P("col", "row"), P("col", "row"), P("col", "row")),
        out_specs=P("col", "row"),
        check_vma=False,
    )
```

time: 175 us -> 84.7 us (0.48)
  blocking collectives: 99.7 us -> 0 us
  Pallas kernels: 0 us -> 82.9 us
  waiting for transfers between devices: 27.3 us -> 0 us
  local copies, waits for them, and re-layouts: 21.5 us -> 1.61 us
  between operations: 13.4 us -> 0.01 us
  matrix products: 12.9 us -> 0 us
    all_to_all x2 -> x0, blocking collectives: 99.7 us -> none  [from_everyone(): lax.all_to_all(jnp.broadcast_to(shard[None], (devices, *shard.shape)), ax...]
    pallas_call x0 -> x1, Pallas kernels: none -> 82.9 us  [body(): pl.pallas_call(kernel, name='precondition', out_shape=jax.ShapeDtypeStruc...]
    all_gather x2 -> x0, waiting for transfers between devices: 25.9 us -> none  [the longest x1 15 us: body(): grad_whole = lax.all_gather(gradient, 'col', axis=0, tiled=True)]
    dot_general x2 -> x0, matrix products: 12.9 us -> none  [the longest x1 7.36 us: body(): jnp.dot(gather_directly(ginv, 'row', 1), rows_part, precision=highest_mod...]
    unnamed x3 -> x1, local copies, waits for them, and re-layouts: 9.49 us -> 1.61 us
    reshape x1 -> x0, local copies, waits for them, and re-layouts: 5.59 us -> none  [joined_along(): return jnp.moveaxis(tiles, 0, dim).reshape(dims)]
    transpose x2 -> x0, local copies, waits for them, and re-layouts: 4.95 us -> none  [joined_along(): return jnp.moveaxis(tiles, 0, dim).reshape(dims)]
  transfers between devices with their start and end apart: 2 -> 0, of which waited for: 2 -> 0; matrix products, arithmetic and copies ran while one was open for 17% -> 0% of each run, Pallas kernels for 0% -> 0%
where the time goes in v1:
time: 84.7 us; the launch traced here: 84.5 us
  Pallas kernels  82.9 us (98%)
  local copies, waits for them, and re-layouts  1.61 us (2%)
    pallas_call x1, Pallas kernels, body(): pl.pallas_call(kernel, name='precondition', out_shape=jax.ShapeDtypeStruc...  82.9 us

profile of v1, /device:TPU:1, one launch (start us, length us, event | category | flops | bytes accessed | tf_op | source)
XLA Modules:
  0.0 84.5 jit_solution(14570246180587250157)
XLA Ops:
  0.0 82.9 %precondition.1 = f32[172,256]{1,0:T(8,128)} custom-call(f32[172,256]{1,0:T(8,128)} %grad_ref.1, f32[172,344]{1,0:T(8,128)} %ginv_ref.1, f32[128,256]{1,0:T(8,128)} %ainv_ref.1), custom_call_target="tpu_custom_call" | custom-call | tf_op jit(solution)/shard_map/precondition/pallas_call | solution.py:364
  82.9 1.6 %copy.5 = f32[172,256]{1,0:T(8,128)} copy(f32[172,256]{1,0:T(8,128)} %precondition.1) | data formatting | bytes 352256
